TPU v7x, 32 devices: a whole 2x2x4 slice. The times are simulated.
32 devices in a mesh: dp: 4 (over z), expert: 4 (over y, x), tensor: 2 (over core).
Axes of the slice: x: 2, y: 2, z: 4, core: 2. Of those that a mesh axis runs over, the one named last changes fastest.
Arguments:
- tokens: bfloat16 [512, 6144], P('dp', 'tensor'), may hold values from -6 to 6
- out_grad: bfloat16 [512, 6144], P('dp', 'tensor'), may hold values from -6 to 6
- router_weight: bfloat16 [6144, 4], P('tensor'), may hold values from -0.078125 to 0.078125
- gate_weight: bfloat16 [4, 6144, 8192], P('expert', 'tensor', 'dp'), may hold values from -0.078125 to 0.078125
- up_weight: bfloat16 [4, 6144, 8192], P('expert', 'tensor', 'dp'), may hold values from -0.078125 to 0.078125
- down_weight: bfloat16 [4, 8192, 6144], P('expert', 'dp', 'tensor'), may hold values from -0.0625 to 0.0625
- expert_index: int32 [512, 2], P('dp'), may hold values from 0 to 3, as said below
- slot_index: int32 [512, 2], P('dp'), may hold values from 0 to 95, as said below
Outputs:
- tokens_grad: bfloat16 [512, 6144], P(('dp', 'expert'), 'tensor')
- router_grad: float32 [6144, 4], P('tensor')
- gate_grad: bfloat16 [4, 6144, 8192], P('expert', 'tensor', 'dp')
- up_grad: bfloat16 [4, 6144, 8192], P('expert', 'tensor', 'dp')
- down_grad: bfloat16 [4, 8192, 6144], P('expert', 'dp', 'tensor')
Inputs may be any that keep to these rules, and one draw needn't show every extreme that they name: `expert_index`: each row names two different experts; in each aligned block of 128 rows no expert is named more than 96 times, and one expert is named exactly 96 times in every block. `slot_index`: entry k of a row is a slot of the expert in entry k of the same row of expert_index; within one aligned block of 128 rows the choices of one expert have distinct slots.
All inputs are finite; a program needn't handle non-finite values.
Results may differ from a plain program's by a relative error of at most 0.025.
Values may be sent and summed in bfloat16 or wider, within the bound.
A program may use at most 128 MiB of HBM per device.

v0:
```python
import jax
import jax.numpy as jnp
from jax import lax
from jax.sharding import PartitionSpec as P

CAP = 96
highest = lax.Precision.HIGHEST


def contract_rows(left_side, right_side):
    return lax.dot_general(
        left_side, right_side, (((0,), (0,)), ((), ())), preferred_element_type=jnp.float32
    )


def contract_cols(left_side, right_side):
    return lax.dot_general(
        left_side, right_side, (((1,), (1,)), ((), ())), preferred_element_type=jnp.float32
    )


def split_parts(values):
    high_part = values.astype(jnp.bfloat16)
    low_part = (values - high_part.astype(jnp.float32)).astype(jnp.bfloat16)
    return (high_part, low_part)


def table_apply(form, table_low, values):
    high_part, low_part = split_parts(values)
    return jnp.einsum(form, table_low, high_part, preferred_element_type=jnp.float32) + jnp.einsum(
        form, table_low, low_part, preferred_element_type=jnp.float32
    )


def slot_table(experts_here, slots_here, expert_id, capacity):
    positions = lax.broadcasted_iota(jnp.int32, (capacity, experts_here.shape[0]), 0)
    first_table = (experts_here[:, 0] == expert_id)[None, :] & (
        slots_here[:, 0][None, :] == positions
    )
    second_table = (experts_here[:, 1] == expert_id)[None, :] & (
        slots_here[:, 1][None, :] == positions
    )
    return (first_table.astype(jnp.float32), second_table.astype(jnp.float32))


def hidden_terms(gate_sum, up_sum, grad_act, slot_prob):
    gate_sigmoid = jax.nn.sigmoid(gate_sum)
    hidden = (gate_sum * gate_sigmoid * up_sum).astype(jnp.bfloat16)
    prob_grad = jnp.sum(hidden.astype(jnp.float32) * grad_act, axis=1)
    act_grad = slot_prob.astype(jnp.float32)[:, None] * grad_act
    grad_gate = (act_grad * up_sum * gate_sigmoid * (1.0 + gate_sum * (1.0 - gate_sigmoid))).astype(
        jnp.bfloat16
    )
    grad_up = (act_grad * gate_sum * gate_sigmoid).astype(jnp.bfloat16)
    return (hidden, grad_gate, grad_up, prob_grad)


def shards(
    tokens, out_grad, router_weight, gate_weight, up_weight, down_weight, expert_index, slot_index
):
    capacity = CAP
    expert_count = router_weight.shape[1]
    expert_id = lax.axis_index("expert")
    logits = lax.psum(jnp.dot(tokens, router_weight, preferred_element_type=jnp.float32), "tensor")
    chosen = jnp.take_along_axis(logits, expert_index, axis=1)
    pick_prob = jnp.stack(
        [jax.nn.sigmoid(chosen[:, 0] - chosen[:, 1]), jax.nn.sigmoid(chosen[:, 1] - chosen[:, 0])],
        axis=1,
    )
    prob_wide = pick_prob.astype(jnp.bfloat16).astype(jnp.float32)
    first_table, second_table = slot_table(expert_index, slot_index, expert_id, capacity)
    select = first_table + second_table
    select_low = select.astype(jnp.bfloat16)
    local_tokens = jnp.dot(select_low, tokens, preferred_element_type=jnp.float32).astype(
        jnp.bfloat16
    )
    local_grads = jnp.dot(select_low, out_grad, preferred_element_type=jnp.float32).astype(
        jnp.bfloat16
    )
    local_prob = (
        jnp.dot(first_table, prob_wide[:, 0], precision=highest)
        + jnp.dot(second_table, prob_wide[:, 1], precision=highest)
    ).astype(jnp.bfloat16)
    slot_tokens, slot_grads, slot_prob = (
        lax.all_gather(local_tokens, "dp", axis=0, tiled=True),
        lax.all_gather(local_grads, "dp", axis=0, tiled=True),
        lax.all_gather(local_prob, "dp", axis=0, tiled=True),
    )
    gate_block = gate_weight[0]
    up_block = up_weight[0]
    down_block = down_weight[0]
    gate_part = jnp.dot(slot_tokens, gate_block, preferred_element_type=jnp.float32)
    up_part = jnp.dot(slot_tokens, up_block, preferred_element_type=jnp.float32)
    grad_part = contract_cols(slot_grads, down_block)
    gate_sum, up_sum, grad_sum = (
        lax.psum(gate_part.astype(jnp.bfloat16), "tensor").astype(jnp.float32),
        lax.psum(up_part.astype(jnp.bfloat16), "tensor").astype(jnp.float32),
        lax.psum(grad_part.astype(jnp.bfloat16), "tensor").astype(jnp.float32),
    )
    hidden, grad_gate, grad_up, prob_grad = hidden_terms(gate_sum, up_sum, grad_sum, slot_prob)
    scaled_grads = (slot_prob.astype(jnp.float32)[:, None] * slot_grads.astype(jnp.float32)).astype(
        jnp.bfloat16
    )
    down_grad = contract_rows(hidden, scaled_grads).astype(jnp.bfloat16)
    gate_grad = contract_rows(slot_tokens, grad_gate).astype(jnp.bfloat16)
    up_grad = contract_rows(slot_tokens, grad_up).astype(jnp.bfloat16)
    slot_dx = contract_cols(grad_gate, gate_block) + contract_cols(grad_up, up_block)
    own_expert = (lax.broadcasted_iota(jnp.int32, (1, expert_count), 1) == expert_id).astype(
        jnp.float32
    )
    row_dx, row_prob = (
        lax.psum_scatter(
            slot_dx.astype(jnp.bfloat16), "dp", scatter_dimension=0, tiled=True
        ).astype(jnp.float32),
        lax.psum_scatter(
            prob_grad.astype(jnp.bfloat16), "dp", scatter_dimension=0, tiled=True
        ).astype(jnp.float32),
    )
    token_dx = table_apply("cn,cd->nd", select_low, row_dx)
    token_prob = table_apply("cn,c->n", select_low, row_prob)
    token_term, prob_rows = (
        lax.psum_scatter(
            token_dx.astype(jnp.bfloat16), "expert", scatter_dimension=0, tiled=True
        ).astype(jnp.float32),
        lax.psum_scatter(
            (token_prob[:, None] * own_expert).astype(jnp.bfloat16),
            "expert",
            scatter_dimension=0,
            tiled=True,
        ).astype(jnp.float32),
    )
    quarter = token_term.shape[0]
    offset = expert_id * quarter
    part_prob = lax.dynamic_slice_in_dim(pick_prob, offset, quarter, 0)
    part_experts = lax.dynamic_slice_in_dim(expert_index, offset, quarter, 0)
    part_tokens = lax.dynamic_slice_in_dim(tokens, offset, quarter, 0)
    pick_grad = jnp.take_along_axis(prob_rows, part_experts, axis=1)
    mixed_grad = jnp.sum(part_prob * pick_grad, axis=1, keepdims=True)
    weights = part_prob * (pick_grad - mixed_grad)
    onehot = (
        part_experts[:, :, None] == lax.broadcasted_iota(jnp.int32, (1, 1, expert_count), 2)
    ).astype(jnp.float32)
    logit_grad = jnp.sum(onehot * weights[:, :, None], axis=1)
    router_rows = router_weight.astype(jnp.float32)
    tokens_grad = (token_term + jnp.dot(logit_grad, router_rows.T, precision=highest)).astype(
        jnp.bfloat16
    )
    router_part = jnp.dot(part_tokens.astype(jnp.float32).T, logit_grad, precision=highest)
    router_grad = lax.psum(router_part, ("dp", "expert"))
    return (tokens_grad, router_grad, gate_grad[None], up_grad[None], down_grad[None])


def solution(mesh):
    in_specs = (
        P("dp", "tensor"),
        P("dp", "tensor"),
        P("tensor", None),
        P("expert", "tensor", "dp"),
        P("expert", "tensor", "dp"),
        P("expert", "dp", "tensor"),
        P("dp", None),
        P("dp", None),
    )
    out_specs = (
        P(("dp", "expert"), "tensor"),
        P("tensor", None),
        P("expert", "tensor", "dp"),
        P("expert", "tensor", "dp"),
        P("expert", "dp", "tensor"),
    )
    return jax.shard_map(shards, mesh=mesh, in_specs=in_specs, out_specs=out_specs, check_vma=False)
```

profile of v0, /device:TPU:0, one launch (start us, length us, event | category | flops | bytes accessed | tf_op | source)
XLA Modules:
  0.0 356.0 jit_solution(7405413484927864889)
XLA Ops:
  7.2 0.8 slice_bitcast_fusion.1
  8.0 0.8 compare_bitcast_fusion.1
  8.8 1.1 convolution_convert_fusion
  10.0 2.3 convolution_convert_fusion.1
  12.3 50.6 %all-gather.5.cloned.1.call-done = bf16[384,3072]{1,0:T(8,128)(2,1)} async-done(((bf16[96,3072]{1,0:T(8,128)(2,1)}), bf16[384,3072]{1,0:T(8,128)(2,1)}) %all-gather.5.cloned.1.call-update) | async-done | bytes 2359312 | tf_op jit(solution)/shard_map/all_gather | solution.py:85
  62.9 11.3 %fusion.31 = bf16[384,2048]{1,0:T(8,128)(2,1)} fusion(bf16[384,3072]{1,0:T(8,128)(2,1)} %all-gather.5.cloned.1.call-done, bf16[1,3072,2048]{2,1,0:T(8,128)(2,1)} %param.11), kind=kOutput, calls=%fused_computation.44 | convolution fusion | flops 4832624640 | bytes 16515072 | tf_op jit(solution)/shard_map/dot_general | solution.py:92
  74.1 9.4 %fusion.28 = bf16[384,2048]{1,0:T(8,128)(2,1)} fusion(bf16[384,3072]{1,0:T(8,128)(2,1)S(1)} %copy-done.8, bf16[1,3072,2048]{2,1,0:T(8,128)(2,1)} %param.12), kind=kOutput, calls=%fused_computation.43 | convolution fusion | flops 4832624640 | bytes 16515072 | tf_op jit(solution)/shard_map/dot_general | solution.py:93
  83.5 30.3 %all-gather.3.cloned.1.call-done = bf16[384,3072]{1,0:T(8,128)(2,1)} async-done(((bf16[96,3072]{1,0:T(8,128)(2,1)}), bf16[384,3072]{1,0:T(8,128)(2,1)}) %all-gather.3.cloned.1.call-update) | async-done | bytes 2359312 | tf_op jit(solution)/shard_map/all_gather | solution.py:86
  113.8 9.6 %fusion.25 = bf16[384,2048]{1,0:T(8,128)(2,1)} fusion(bf16[384,3072]{1,0:T(8,128)(2,1)} %all-gather.3.cloned.1.call-done, bf16[1,2048,3072]{2,1,0:T(8,128)(2,1)} %param.13), kind=kOutput, calls=%fused_computation.42 | convolution fusion | flops 4832624640 | bytes 16515072 | tf_op jit(solution)/shard_map/dot_general | solution.py:17
  123.5 0.6 copy-done.6
  124.4 0.3 fusion.66
  124.7 2.5 psum.35
  127.2 2.4 gather_fusion
  129.7 0.6 fusion.65
  131.5 20.0 %all-reduce.6.cloned.1.call-done = (bf16[384,2048]{1,0:T(8,128)(2,1)}, bf16[384,2048]{1,0:T(8,128)(2,1)}, bf16[384,2048]{1,0:T(8,128)(2,1)}) async-done(((bf16[384,2048]{1,0:T(8,128)(2,1)}, bf16[384,2048]{1,0:T(8,128)(2,1)}, bf16[384,2048]{1,0:T(8,128)(2,1)}), (bf16[384,2048]{1,0:T(8,128)(2,1)}, bf16[384,2048]{1,0:T(8,128)(2,1)}, bf16[384,2048]{1,0:T(8,128)(2,1)})) %all-reduce.6.cloned.1.call-update) | async-done | bytes 4718608 | tf_op jit(solution)/shard_map/psum | solution.py:98
  151.5 3.7 %fusion.14 = bf16[384]{0:T(512)(128)(2,1)S(1)} fusion(bf16[384,2048]{1,0:T(8,128)(2,1)} %get-tuple-element.7, bf16[384,2048]{1,0:T(8,128)(2,1)} %get-tuple-element.8, bf16[384,2048]{1,0:T(8,128)(2,1)} %get-tuple-element.9), kind=kLoop, calls=%fused_computation.31 | loop fusion | flops 9436800 | bytes 4719360 | tf_op jit(solution)/shard_map/reduce_sum | solution.py:49
  155.2 12.1 %all-reduce.2 = (bf16[384]{0:T(512)(128)(2,1)S(1)}, bf16[384]{0:T(512)(128)(2,1)S(1)}) all-reduce(bf16[384]{0:T(512)(128)(2,1)S(1)} %fusion.14, bf16[384]{0:T(512)(128)(2,1)S(1)} %dynamic-update-slice), channel_id=4, replica_groups=mesh['dp'=4,'expert'=4,'tensor'=2] {'dp'}, use_global_device_ids=true, to_apply=%region_7.8.clone | all-reduce | flops 768 | bytes 3072
  167.4 12.2 %fusion = f32[384,3072]{1,0:T(8,128)} fusion(bf16[1,3072,2048]{2,1,0:T(8,128)(2,1)} %param.11, bf16[384,2048]{1,0:T(8,128)(2,1)S(1)} %copy-done.1, bf16[384,2048]{1,0:T(8,128)(2,1)} %get-tuple-element.7, bf16[384,2048]{1,0:T(8,128)(2,1)} %get-tuple-element.9, f32[384]{0:T(512)S(1)} %convert_element_type.124), kind=kOutput, calls=%fused_computation.2 | convolution fusion | flops 4842848256 | bytes 22021632 | tf_op jit(solution)/shard_map/dot_general | solution.py:17
  179.6 16.1 %add_convert_fusion = bf16[384,3072]{1,0:T(8,128)(2,1)} fusion(f32[384,3072]{1,0:T(8,128)} %fusion, bf16[1,3072,2048]{2,1,0:T(8,128)(2,1)} %param.12, bf16[384,2048]{1,0:T(8,128)(2,1)S(1)} %copy-done.2, bf16[384,2048]{1,0:T(8,128)(2,1)} %get-tuple-element.7, f32[384]{0:T(512)S(1)} %convert_element_type.124), kind=kOutput, calls=%fused_computation.20 | convolution fusion | flops 4841275392 | bytes 22808064 | tf_op jit(solution)/shard_map/dot_general | solution.py:17
  197.2 0.7 copy.63
  198.0 0.3 reduce-scatter.8.cloned.1.call-start
  198.3 13.5 %convert_bitcast_fusion.2 = bf16[1,3072,2048]{2,1,0:T(8,128)(2,1)} fusion(bf16[384,3072]{1,0:T(8,128)(2,1)} %all-gather.5.cloned.1.call-done, bf16[384,2048]{1,0:T(8,128)(2,1)S(1)} %copy-done.1, bf16[384,2048]{1,0:T(8,128)(2,1)} %get-tuple-element.7, bf16[384,2048]{1,0:T(8,128)(2,1)} %get-tuple-element.9, f32[384]{0:T(512)S(1)} %convert_element_type.124), kind=kOutput, calls=%fused_computation.14 | convolution fusion | flops 4849139712 | bytes 19662336 | tf_op jit(solution)/shard_map/dot_general | solution.py:11
  211.8 10.3 %convert_bitcast_fusion.1 = bf16[1,3072,2048]{2,1,0:T(8,128)(2,1)} fusion(bf16[384,3072]{1,0:T(8,128)(2,1)S(1)} %copy-done.9, bf16[384,2048]{1,0:T(8,128)(2,1)S(1)} %copy-done.3, bf16[384,2048]{1,0:T(8,128)(2,1)S(1)} %copy-done.4, f32[384]{0:T(512)S(1)} %convert_element_type.124), kind=kOutput, calls=%fused_computation.13 | convolution fusion | flops 4845207552 | bytes 18089472 | tf_op jit(solution)/shard_map/dot_general | solution.py:11
  222.1 19.6 %reduce-scatter.6.cloned.1.call-done = bf16[96,3072]{1,0:T(8,128)(2,1)} async-done(((bf16[384,3072]{1,0:T(8,128)(2,1)}), bf16[96,3072]{1,0:T(8,128)(2,1)}) %reduce-scatter.6.cloned.1.call-update) | async-done | bytes 589840 | tf_op jit(solution)/shard_map/reduce_scatter | solution.py:112
  241.8 1.5 fusion.48
  243.2 2.4 fusion.12
  245.6 12.1 %convert_bitcast_fusion = bf16[1,2048,3072]{2,1,0:T(8,128)(2,1)} fusion(bf16[384,3072]{1,0:T(8,128)(2,1)} %all-gather.3.cloned.1.call-done, f32[384]{0:T(512)S(1)} %convert_element_type.124, bf16[384,2048]{1,0:T(8,128)(2,1)S(1)} %copy-done.1, bf16[384,2048]{1,0:T(8,128)(2,1)} %get-tuple-element.9), kind=kOutput, calls=%fused_computation.12 | convolution fusion | flops 4847960064 | bytes 18089472 | tf_op jit(solution)/shard_map/dot_general | solution.py:11
  257.7 10.6 %reduce-scatter.10.cloned.1.call-done = bf16[32,4]{1,0:T(8,128)(2,1)} async-done(((bf16[128,4]{1,0:T(8,128)(2,1)}), bf16[32,4]{1,0:T(8,128)(2,1)}) %reduce-scatter.10.cloned.1.call-update) | async-done | bytes 272
  268.4 0.8 copy.64
  269.2 0.9 gather_fusion.1
  270.6 76.5 %psum.39 = f32[3072,4]{0,1:T(4,128)} all-reduce(f32[3072,4]{0,1:T(4,128)S(1)} %fusion.38), channel_id=1, replica_groups=mesh['dp'=4,'expert'=4,'tensor'=2] {'dp','expert'}, use_global_device_ids=true, to_apply=%region_11.12 | all-reduce | flops 12288 | bytes 98304 | tf_op jit(solution)/shard_map/psum | solution.py:149
  347.1 2.0 fusion.13
  (59 shorter events, 2.6 us)
Async XLA Ops:
  7.2 1.6 copy-start
  7.2 55.7 %all-gather.5.cloned.1.call-start = ((), (), s32[]{:S(2)}) async-start(), calls=%async_computation.4 | async-start | bytes 2949120 | tf_op jit(solution)/shard_map/all_gather | solution.py:85
  9.9 103.9 %all-gather.3.cloned.1.call-start = ((), (), s32[]{:S(2)}) async-start(), calls=%async_computation.3 | async-start | bytes 2949120 | tf_op jit(solution)/shard_map/all_gather | solution.py:86
  12.3 139.3 %all-reduce.6.cloned.1.call-start = ((), (), s32[]{:S(2)}) async-start(), calls=%async_computation.8 | async-start | bytes 9437184 | tf_op jit(solution)/shard_map/psum | solution.py:98
  62.9 11.3 %copy-start.8 = (bf16[384,3072]{1,0:T(8,128)(2,1)S(1)}, bf16[384,3072]{1,0:T(8,128)(2,1)}, u32[]{:S(2)}) copy-start(bf16[384,3072]{1,0:T(8,128)(2,1)} %all-gather.5.cloned.1.call-done) | copy-start | bytes 7077892
  123.4 0.7 copy-start.6
  123.4 0.9 copy-start.5
  123.5 118.3 %reduce-scatter.6.cloned.1.call-start = ((), (), s32[]{:S(2)}) async-start(), calls=%async_computation.5 | async-start | bytes 2949120 | tf_op jit(solution)/shard_map/reduce_scatter | solution.py:112
  127.2 2.6 copy-start.7
  151.5 15.8 %copy-start.1 = (bf16[384,2048]{1,0:T(8,128)(2,1)S(1)}, bf16[384,2048]{1,0:T(8,128)(2,1)}, u32[]{:S(2)}) copy-start(bf16[384,2048]{1,0:T(8,128)(2,1)} %get-tuple-element.8) | copy-start | bytes 4718596
  167.4 12.2 %copy-start.2 = (bf16[384,2048]{1,0:T(8,128)(2,1)S(1)}, bf16[384,2048]{1,0:T(8,128)(2,1)}, u32[]{:S(2)}) copy-start(bf16[384,2048]{1,0:T(8,128)(2,1)} %get-tuple-element.9) | copy-start | bytes 4718596
  195.7 72.6 %reduce-scatter.10.cloned.1.call-start = ((), (), s32[]{:S(2)}) async-start(), calls=%async_computation.7 | async-start | bytes 40960
  198.0 149.2 %reduce-scatter.8.cloned.1.call-start = ((), (), s32[]{:S(2)}) async-start(), calls=%async_computation.6 | async-start | bytes 983040 | tf_op jit(solution)/shard_map/reduce_scatter | solution.py:122
  198.2 13.5 %copy-start.3 = (bf16[384,2048]{1,0:T(8,128)(2,1)S(1)}, bf16[384,2048]{1,0:T(8,128)(2,1)}, u32[]{:S(2)}) copy-start(bf16[384,2048]{1,0:T(8,128)(2,1)} %get-tuple-element.9) | copy-start | bytes 4718596
  198.3 13.5 %copy-start.4 = (bf16[384,2048]{1,0:T(8,128)(2,1)S(1)}, bf16[384,2048]{1,0:T(8,128)(2,1)}, u32[]{:S(2)}) copy-start(bf16[384,2048]{1,0:T(8,128)(2,1)} %get-tuple-element.7) | copy-start | bytes 4718596
  198.3 13.5 %copy-start.9 = (bf16[384,3072]{1,0:T(8,128)(2,1)S(1)}, bf16[384,3072]{1,0:T(8,128)(2,1)}, u32[]{:S(2)}) copy-start(bf16[384,3072]{1,0:T(8,128)(2,1)} %all-gather.5.cloned.1.call-done) | copy-start | bytes 7077892
Sparse Core Ops, SparseCore 0:
  10.1 52.6 all-gather.4
  65.0 48.7 all-gather.2
  123.6 27.9 all-reduce.5
  195.9 45.8 reduce-scatter.5
  244.9 23.4 reduce-scatter.9
  271.1 26.3 reduce-scatter.7
where the time goes:
time: 356 us
  waiting for transfers between devices  131 us (37%)
  matrix products  105 us (29%)
  blocking collectives  91.1 us (26%)
  between operations  15.6 us (4%)
  local copies, waits for them, and re-layouts  7.8 us (2%)
  other arithmetic  4.83 us (1%)
    psum x1, blocking collectives, shards(): router_grad = lax.psum(router_part, ('dp', 'expert'))  76.5 us
    all_gather x1, waiting for transfers between devices, shards(): lax.all_gather(local_tokens, 'dp', axis=0, tiled=True)  50.6 us
    dot_general x3, matrix products, contract_cols(): lax.dot_general(left_side, right_side, (((1,), (1,)), ((), ())), preferre...  38 us
    dot_general x3, matrix products, contract_rows(): lax.dot_general(left_side, right_side, (((0,), (0,)), ((), ())), preferre...  36 us
    all_gather x1, waiting for transfers between devices, shards(): lax.all_gather(local_grads, 'dp', axis=0, tiled=True)  30.3 us
    psum x1, waiting for transfers between devices, shards(): lax.psum(grad_part.astype(jnp.bfloat16), 'tensor').astype(jnp.float32)  20 us
    reduce_scatter x1, waiting for transfers between devices, shards(): lax.psum_scatter(slot_dx.astype(jnp.bfloat16), 'dp', scatter_dimension=0,...  19.6 us
    unnamed x1, blocking collectives  12.1 us
  transfers between devices with their start and end apart: 6, of which 5 were waited for; matrix products, arithmetic and copies ran while one was open for 20% of the time, Pallas kernels for 0%

commit v1 on v0

--- a/solution.py
+++ b/solution.py
@@ -146,7 +146,8 @@
         jnp.bfloat16
     )
     router_part = jnp.dot(part_tokens.astype(jnp.float32).T, logit_grad, precision=highest)
-    router_grad = lax.psum(router_part, ("dp", "expert"))
+    parts = lax.all_gather(router_part, ("dp", "expert"))
+    router_grad = jnp.sum(parts, axis=0)
     return (tokens_grad, router_grad, gate_grad[None], up_grad[None], down_grad[None])
 
 

time: 356 us -> 326 us (0.916)
  blocking collectives: 91.1 us -> 59.5 us
    psum x1 -> x0, blocking collectives: 76.5 us -> none  [shards(): router_grad = lax.psum(router_part, ('dp', 'expert'))]
    all_gather x0 -> x1, blocking collectives: none -> 44.9 us  [shards(): parts = lax.all_gather(router_part, ('dp', 'expert'))]
  transfers between devices with their start and end apart: 6 -> 6, of which waited for: 5 -> 5; matrix products, arithmetic and copies ran while one was open for 20% -> 22% of each run, Pallas kernels for 0% -> 0%
where the time goes in v1:
time: 326 us; the launch traced here: 325 us
  waiting for transfers between devices  131 us (40%)
  matrix products  105 us (32%)
  blocking collectives  59.5 us (18%)
  between operations  15.6 us (5%)
  local copies, waits for them, and re-layouts  7.8 us (2%)
  other arithmetic  5.97 us (2%)
    all_gather x1, waiting for transfers between devices, shards(): lax.all_gather(local_tokens, 'dp', axis=0, tiled=True)  50.6 us
    all_gather x1, blocking collectives, shards(): parts = lax.all_gather(router_part, ('dp', 'expert'))  44.9 us
    dot_general x3, matrix products, contract_cols(): lax.dot_general(left_side, right_side, (((1,), (1,)), ((), ())), preferre...  38 us
    dot_general x3, matrix products, contract_rows(): lax.dot_general(left_side, right_side, (((0,), (0,)), ((), ())), preferre...  36 us
    all_gather x1, waiting for transfers between devices, shards(): lax.all_gather(local_grads, 'dp', axis=0, tiled=True)  30.3 us
    psum x1, waiting for transfers between devices, shards(): lax.psum(grad_part.astype(jnp.bfloat16), 'tensor').astype(jnp.float32)  20 us
    reduce_scatter x1, waiting for transfers between devices, shards(): lax.psum_scatter(slot_dx.astype(jnp.bfloat16), 'dp', scatter_dimension=0,...  19.6 us
    unnamed x1, blocking collectives  12.1 us
  transfers between devices with their start and end apart: 6, of which 5 were waited for; matrix products, arithmetic and copies ran while one was open for 22% of the time, Pallas kernels for 0%

profile of v1, /device:TPU:0, one launch (start us, length us, event | category | flops | bytes accessed | tf_op | source)
XLA Modules:
  0.0 325.5 jit_solution(13892244223146294197)
XLA Ops:
  7.2 0.8 slice_bitcast_fusion.1
  8.0 0.8 compare_bitcast_fusion.1
  8.8 1.1 convolution_convert_fusion
  10.0 2.3 convolution_convert_fusion.1
  12.3 50.6 %all-gather.6.cloned.1.call-done = bf16[384,3072]{1,0:T(8,128)(2,1)} async-done(((bf16[96,3072]{1,0:T(8,128)(2,1)}), bf16[384,3072]{1,0:T(8,128)(2,1)}) %all-gather.6.cloned.1.call-update) | async-done | bytes 2359312 | tf_op jit(solution)/shard_map/all_gather | solution.py:85
  62.9 11.3 %fusion.31 = bf16[384,2048]{1,0:T(8,128)(2,1)} fusion(bf16[384,3072]{1,0:T(8,128)(2,1)} %all-gather.6.cloned.1.call-done, bf16[1,3072,2048]{2,1,0:T(8,128)(2,1)} %param.11), kind=kOutput, calls=%fused_computation.44 | convolution fusion | flops 4832624640 | bytes 16515072 | tf_op jit(solution)/shard_map/dot_general | solution.py:92
  74.1 9.4 %fusion.28 = bf16[384,2048]{1,0:T(8,128)(2,1)} fusion(bf16[384,3072]{1,0:T(8,128)(2,1)S(1)} %copy-done.8, bf16[1,3072,2048]{2,1,0:T(8,128)(2,1)} %param.12), kind=kOutput, calls=%fused_computation.43 | convolution fusion | flops 4832624640 | bytes 16515072 | tf_op jit(solution)/shard_map/dot_general | solution.py:93
  83.5 30.3 %all-gather.4.cloned.1.call-done = bf16[384,3072]{1,0:T(8,128)(2,1)} async-done(((bf16[96,3072]{1,0:T(8,128)(2,1)}), bf16[384,3072]{1,0:T(8,128)(2,1)}) %all-gather.4.cloned.1.call-update) | async-done | bytes 2359312 | tf_op jit(solution)/shard_map/all_gather | solution.py:86
  113.8 9.6 %fusion.25 = bf16[384,2048]{1,0:T(8,128)(2,1)} fusion(bf16[384,3072]{1,0:T(8,128)(2,1)} %all-gather.4.cloned.1.call-done, bf16[1,2048,3072]{2,1,0:T(8,128)(2,1)} %param.13), kind=kOutput, calls=%fused_computation.42 | convolution fusion | flops 4832624640 | bytes 16515072 | tf_op jit(solution)/shard_map/dot_general | solution.py:17
  123.5 0.6 copy-done.6
  124.4 0.3 fusion.66
  124.7 2.5 psum.28
  127.2 2.4 gather_fusion
  129.7 0.6 fusion.65
  131.5 20.0 %all-reduce.6.cloned.1.call-done = (bf16[384,2048]{1,0:T(8,128)(2,1)}, bf16[384,2048]{1,0:T(8,128)(2,1)}, bf16[384,2048]{1,0:T(8,128)(2,1)}) async-done(((bf16[384,2048]{1,0:T(8,128)(2,1)}, bf16[384,2048]{1,0:T(8,128)(2,1)}, bf16[384,2048]{1,0:T(8,128)(2,1)}), (bf16[384,2048]{1,0:T(8,128)(2,1)}, bf16[384,2048]{1,0:T(8,128)(2,1)}, bf16[384,2048]{1,0:T(8,128)(2,1)})) %all-reduce.6.cloned.1.call-update) | async-done | bytes 4718608 | tf_op jit(solution)/shard_map/psum | solution.py:98
  151.5 3.7 %fusion.14 = bf16[384]{0:T(512)(128)(2,1)S(1)} fusion(bf16[384,2048]{1,0:T(8,128)(2,1)} %get-tuple-element.7, bf16[384,2048]{1,0:T(8,128)(2,1)} %get-tuple-element.8, bf16[384,2048]{1,0:T(8,128)(2,1)} %get-tuple-element.9), kind=kLoop, calls=%fused_computation.31 | loop fusion | flops 9436800 | bytes 4719360 | tf_op jit(solution)/shard_map/reduce_sum | solution.py:49
  155.2 12.1 %all-reduce.2 = (bf16[384]{0:T(512)(128)(2,1)S(1)}, bf16[384]{0:T(512)(128)(2,1)S(1)}) all-reduce(bf16[384]{0:T(512)(128)(2,1)S(1)} %fusion.14, bf16[384]{0:T(512)(128)(2,1)S(1)} %dynamic-update-slice), channel_id=5, replica_groups=mesh['dp'=4,'expert'=4,'tensor'=2] {'dp'}, use_global_device_ids=true, to_apply=%region_7.8.clone | all-reduce | flops 768 | bytes 3072
  167.4 12.2 %fusion = f32[384,3072]{1,0:T(8,128)} fusion(bf16[1,3072,2048]{2,1,0:T(8,128)(2,1)} %param.11, bf16[384,2048]{1,0:T(8,128)(2,1)S(1)} %copy-done.1, bf16[384,2048]{1,0:T(8,128)(2,1)} %get-tuple-element.7, bf16[384,2048]{1,0:T(8,128)(2,1)} %get-tuple-element.9, f32[384]{0:T(512)S(1)} %convert_element_type.124), kind=kOutput, calls=%fused_computation.2 | convolution fusion | flops 4842848256 | bytes 22021632 | tf_op jit(solution)/shard_map/dot_general | solution.py:17
  179.6 16.1 %add_convert_fusion = bf16[384,3072]{1,0:T(8,128)(2,1)} fusion(f32[384,3072]{1,0:T(8,128)} %fusion, bf16[1,3072,2048]{2,1,0:T(8,128)(2,1)} %param.12, bf16[384,2048]{1,0:T(8,128)(2,1)S(1)} %copy-done.2, bf16[384,2048]{1,0:T(8,128)(2,1)} %get-tuple-element.7, f32[384]{0:T(512)S(1)} %convert_element_type.124), kind=kOutput, calls=%fused_computation.20 | convolution fusion | flops 4841275392 | bytes 22808064 | tf_op jit(solution)/shard_map/dot_general | solution.py:17
  197.2 0.7 copy.63
  198.3 13.5 %convert_bitcast_fusion.2 = bf16[1,3072,2048]{2,1,0:T(8,128)(2,1)} fusion(bf16[384,3072]{1,0:T(8,128)(2,1)} %all-gather.6.cloned.1.call-done, bf16[384,2048]{1,0:T(8,128)(2,1)S(1)} %copy-done.1, bf16[384,2048]{1,0:T(8,128)(2,1)} %get-tuple-element.7, bf16[384,2048]{1,0:T(8,128)(2,1)} %get-tuple-element.9, f32[384]{0:T(512)S(1)} %convert_element_type.124), kind=kOutput, calls=%fused_computation.14 | convolution fusion | flops 4849139712 | bytes 19662336 | tf_op jit(solution)/shard_map/dot_general | solution.py:11
  211.8 10.3 %convert_bitcast_fusion.1 = bf16[1,3072,2048]{2,1,0:T(8,128)(2,1)} fusion(bf16[384,3072]{1,0:T(8,128)(2,1)S(1)} %copy-done.9, bf16[384,2048]{1,0:T(8,128)(2,1)S(1)} %copy-done.3, bf16[384,2048]{1,0:T(8,128)(2,1)S(1)} %copy-done.4, f32[384]{0:T(512)S(1)} %convert_element_type.124), kind=kOutput, calls=%fused_computation.13 | convolution fusion | flops 4845207552 | bytes 18089472 | tf_op jit(solution)/shard_map/dot_general | solution.py:11
  222.1 19.6 %reduce-scatter.6.cloned.1.call-done = bf16[96,3072]{1,0:T(8,128)(2,1)} async-done(((bf16[384,3072]{1,0:T(8,128)(2,1)}), bf16[96,3072]{1,0:T(8,128)(2,1)}) %reduce-scatter.6.cloned.1.call-update) | async-done | bytes 589840 | tf_op jit(solution)/shard_map/reduce_scatter | solution.py:112
  241.8 1.5 fusion.48
  243.2 2.4 fusion.12
  245.6 12.1 %convert_bitcast_fusion = bf16[1,2048,3072]{2,1,0:T(8,128)(2,1)} fusion(bf16[384,3072]{1,0:T(8,128)(2,1)} %all-gather.4.cloned.1.call-done, f32[384]{0:T(512)S(1)} %convert_element_type.124, bf16[384,2048]{1,0:T(8,128)(2,1)S(1)} %copy-done.1, bf16[384,2048]{1,0:T(8,128)(2,1)} %get-tuple-element.9), kind=kOutput, calls=%fused_computation.12 | convolution fusion | flops 4847960064 | bytes 18089472 | tf_op jit(solution)/shard_map/dot_general | solution.py:11
  257.7 10.6 %reduce-scatter.10.cloned.1.call-done = bf16[32,4]{1,0:T(8,128)(2,1)} async-done(((bf16[128,4]{1,0:T(8,128)(2,1)}), bf16[32,4]{1,0:T(8,128)(2,1)}) %reduce-scatter.10.cloned.1.call-update) | async-done | bytes 272
  268.4 0.8 copy.64
  269.2 0.9 gather_fusion.1
  270.6 44.9 %all-gather = f32[49152,4]{0,1:T(4,128)S(1)} all-gather(f32[3072,4]{0,1:T(4,128)S(1)} %fusion.38), channel_id=2, replica_groups=mesh['dp'=4,'expert'=4,'tensor'=2] {'dp','expert'}, dimensions={0}, use_global_device_ids=true | all-gather | bytes 835584 | tf_op jit(solution)/shard_map/all_gather | solution.py:149
  315.5 1.1 bitcast_reduce_fusion
  316.6 2.0 fusion.13
  (60 shorter events, 2.9 us)
Async XLA Ops:
  7.2 1.6 copy-start
  7.2 55.7 %all-gather.6.cloned.1.call-start = ((), (), s32[]{:S(2)}) async-start(), calls=%async_computation.4 | async-start | bytes 2949120 | tf_op jit(solution)/shard_map/all_gather | solution.py:85
  9.9 103.9 %all-gather.4.cloned.1.call-start = ((), (), s32[]{:S(2)}) async-start(), calls=%async_computation.3 | async-start | bytes 2949120 | tf_op jit(solution)/shard_map/all_gather | solution.py:86
  12.3 139.3 %all-reduce.6.cloned.1.call-start = ((), (), s32[]{:S(2)}) async-start(), calls=%async_computation.8 | async-start | bytes 9437184 | tf_op jit(solution)/shard_map/psum | solution.py:98
  62.9 11.3 %copy-start.8 = (bf16[384,3072]{1,0:T(8,128)(2,1)S(1)}, bf16[384,3072]{1,0:T(8,128)(2,1)}, u32[]{:S(2)}) copy-start(bf16[384,3072]{1,0:T(8,128)(2,1)} %all-gather.6.cloned.1.call-done) | copy-start | bytes 7077892
  123.4 0.7 copy-start.6
  123.4 0.9 copy-start.5
  123.5 118.3 %reduce-scatter.6.cloned.1.call-start = ((), (), s32[]{:S(2)}) async-start(), calls=%async_computation.5 | async-start | bytes 2949120 | tf_op jit(solution)/shard_map/reduce_scatter | solution.py:112
  127.2 2.6 copy-start.7
  151.5 15.8 %copy-start.1 = (bf16[384,2048]{1,0:T(8,128)(2,1)S(1)}, bf16[384,2048]{1,0:T(8,128)(2,1)}, u32[]{:S(2)}) copy-start(bf16[384,2048]{1,0:T(8,128)(2,1)} %get-tuple-element.8) | copy-start | bytes 4718596
  167.4 12.2 %copy-start.2 = (bf16[384,2048]{1,0:T(8,128)(2,1)S(1)}, bf16[384,2048]{1,0:T(8,128)(2,1)}, u32[]{:S(2)}) copy-start(bf16[384,2048]{1,0:T(8,128)(2,1)} %get-tuple-element.9) | copy-start | bytes 4718596
  195.7 72.6 %reduce-scatter.10.cloned.1.call-start = ((), (), s32[]{:S(2)}) async-start(), calls=%async_computation.7 | async-start | bytes 40960
  198.0 118.7 %reduce-scatter.8.cloned.1.call-start = ((), (), s32[]{:S(2)}) async-start(), calls=%async_computation.6 | async-start | bytes 983040 | tf_op jit(solution)/shard_map/reduce_scatter | solution.py:122
  198.2 13.5 %copy-start.3 = (bf16[384,2048]{1,0:T(8,128)(2,1)S(1)}, bf16[384,2048]{1,0:T(8,128)(2,1)}, u32[]{:S(2)}) copy-start(bf16[384,2048]{1,0:T(8,128)(2,1)} %get-tuple-element.9) | copy-start | bytes 4718596
  198.3 13.5 %copy-start.4 = (bf16[384,2048]{1,0:T(8,128)(2,1)S(1)}, bf16[384,2048]{1,0:T(8,128)(2,1)}, u32[]{:S(2)}) copy-start(bf16[384,2048]{1,0:T(8,128)(2,1)} %get-tuple-element.7) | copy-start | bytes 4718596
  198.3 13.5 %copy-start.9 = (bf16[384,3072]{1,0:T(8,128)(2,1)S(1)}, bf16[384,3072]{1,0:T(8,128)(2,1)}, u32[]{:S(2)}) copy-start(bf16[384,3072]{1,0:T(8,128)(2,1)} %all-gather.6.cloned.1.call-done) | copy-start | bytes 7077892
Sparse Core Ops, SparseCore 0:
  10.1 52.6 all-gather.5
  65.0 48.7 all-gather.3
  123.6 27.9 all-reduce.5
  195.9 45.8 reduce-scatter.5
  244.9 23.4 reduce-scatter.9
  271.1 30.2 reduce-scatter.7
